TPU v7x, 32 devices: a whole 2x2x4 slice. The times are simulated.
32 devices in a mesh: pop: 8 (over z, y), mp: 4 (over x, core).
Axes of the slice: x: 2, y: 2, z: 4, core: 2. Of those that a mesh axis runs over, the one named last changes fastest.
Arguments:
- token_ids: int32 [96, 4, 16], P('pop'), may hold values from 0 to 255
- fitness_ranks: int32 [96], P('pop'), may hold values from 0 to 143, as said below
- embedding: bfloat16 [256, 4096], P(None, 'mp'), may hold values from -6 to 6
- mix_weights: bfloat16 [2, 4096, 4096], P(None, 'mp'), may hold values from -0.09375 to 0.09375
- factors_in: bfloat16 [2, 96, 4, 4096], P(None, 'pop', None, 'mp'), may hold values from -6 to 6
- factors_out: bfloat16 [2, 96, 4, 4096], P(None, 'pop'), may hold values from -6 to 6
- decay_rates: float32 [2, 4096], P(None, 'mp'), may hold values from 0.2 to 0.98
- norm_gain: float32 [2, 4096], P(None, 'mp'), may hold values from 0.1 to 1.9
- reward_dir: float32 [4096], P('mp'), may hold values from -6 to 6
Outputs:
- final_features: bfloat16 [96, 4, 4096], P('pop', None, 'mp')
- scores: float32 [96, 4], P('pop')
- weight_step: float32 [2, 4096, 4096], P(None, 'mp', 'pop')
Inputs may be any that keep to these rules, and one draw needn't show every extreme that they name: `fitness_ranks`: ranks may repeat.
All inputs are finite; a program needn't handle non-finite values.
Results may differ from a plain program's by a relative error of at most 0.023.
Values may be sent and summed in bfloat16 or wider, within the bound.
A program may use at most 128 MiB of HBM per device.

v0:
```python
import jax
import jax.numpy as jnp
from jax import lax
from jax.sharding import PartitionSpec as P

noise_scale = 0.25
norm_eps = 1e-06
spread_eps = 1e-05


def recurrence(inputs, decay):
    carried = jnp.zeros(inputs.shape[1:], jnp.float32)
    states = []
    for step in range(inputs.shape[0]):
        carried = decay * carried + (1.0 - decay) * inputs[step]
        states.append(carried)
    return jnp.stack(states, axis=0)


def mixed_inputs(hidden, weight_rows):
    flat = hidden.reshape(-1, hidden.shape[-1])
    partial_value = jnp.dot(flat, weight_rows, preferred_element_type=jnp.float32)
    summed = lax.psum_scatter(
        partial_value.astype(jnp.bfloat16), "mp", scatter_dimension=1, tiled=True
    ).astype(jnp.float32)
    return summed


def project_rank(hidden, factor_rows):
    return jnp.einsum("tmsd,mrd->tmsr", hidden, factor_rows, preferred_element_type=jnp.float32)


def shards(
    token_ids,
    fitness_ranks,
    embedding,
    mix_weights,
    factors_in,
    factors_out,
    decay_rates,
    norm_gain,
    reward_dir,
):
    members, seq_count, step_count = token_ids.shape
    local_width = embedding.shape[1]
    vocab_size = embedding.shape[0]
    layers = mix_weights.shape[0]
    full_width = mix_weights.shape[2]
    rank_count = factors_in.shape[2]
    pop_count = lax.axis_size("pop")
    members_all = members * pop_count
    coef = noise_scale * (full_width * rank_count) ** (-0.5)
    position = lax.axis_index("mp")
    outputs_local = lax.dynamic_slice_in_dim(
        factors_out, position * local_width, local_width, 3
    ).astype(jnp.float32)
    onehot = (
        jnp.moveaxis(token_ids, 2, 0).reshape(-1)[:, None]
        == jnp.arange(vocab_size, dtype=jnp.int32)[None, :]
    ).astype(jnp.bfloat16)
    hidden = jnp.dot(onehot, embedding, preferred_element_type=jnp.float32).astype(jnp.bfloat16)
    hidden = hidden.reshape(step_count, members, seq_count, local_width)
    for layer_idx in range(layers):
        if layer_idx == 0:
            table = mixed_inputs(embedding, mix_weights[0])
            top = table.astype(jnp.bfloat16)
            rest = (table - top.astype(jnp.float32)).astype(jnp.bfloat16)
            base_mix = jnp.dot(onehot, top, preferred_element_type=jnp.float32) + jnp.dot(
                onehot, rest, preferred_element_type=jnp.float32
            )
        else:
            base_mix = mixed_inputs(hidden, mix_weights[layer_idx])
        base_mix = base_mix.reshape(hidden.shape)
        low_rank = lax.psum(project_rank(hidden, factors_in[layer_idx]), "mp")
        correction = jnp.einsum(
            "tmsr,mrd->tmsd", low_rank, outputs_local[layer_idx], precision=lax.Precision.HIGHEST
        )
        states = recurrence(base_mix + coef * correction, decay_rates[layer_idx])
        squares = lax.psum(jnp.sum(states * states, axis=3), "mp")
        norm_scale = lax.rsqrt(squares / full_width + norm_eps)
        hidden = (
            hidden.astype(jnp.float32) + states * norm_scale[..., None] * norm_gain[layer_idx]
        ).astype(jnp.bfloat16)
    dots_local = jnp.einsum(
        "tmsd,d->tms", hidden.astype(jnp.float32), reward_dir, precision=lax.Precision.HIGHEST
    )
    reward_terms = lax.psum(dots_local, "mp")
    final_features = hidden[step_count - 1]
    scores = jnp.mean(reward_terms, axis=0) * full_width ** (-0.5)
    ranks_every = lax.all_gather(fitness_ranks, "pop", axis=0, tiled=True)
    shares_all = ranks_every.astype(jnp.float32) / members_all
    rank_mean = jnp.mean(shares_all)
    rank_spread = jnp.mean((shares_all - rank_mean) * (shares_all - rank_mean)) + spread_eps
    shaped_all = (shares_all - rank_mean) * lax.rsqrt(rank_spread)
    columns = lax.all_to_all(factors_out, "pop", split_axis=3, concat_axis=1, tiled=True)
    weighted = (
        lax.all_gather(factors_in, "pop", axis=1, tiled=True).astype(jnp.float32)
        * shaped_all[None, :, None, None]
    ).astype(jnp.bfloat16)
    weight_delta = jnp.einsum(
        "lmri,lmro->lio", weighted, columns, preferred_element_type=jnp.float32
    )
    weight_step = weight_delta * (members_all * rank_count) ** (-0.5)
    return (final_features, scores, weight_step)


def solution(mesh):
    return jax.shard_map(
        shards,
        mesh=mesh,
        in_specs=(
            P("pop", None, None),
            P("pop"),
            P(None, "mp"),
            P(None, "mp", None),
            P(None, "pop", None, "mp"),
            P(None, "pop", None, None),
            P(None, "mp"),
            P(None, "mp"),
            P("mp"),
        ),
        out_specs=(P("pop", None, "mp"), P("pop", None), P(None, "mp", "pop")),
        check_vma=False,
    )
```

profile of v0, /device:TPU:0, one launch (start us, length us, event | category | flops | bytes accessed | tf_op | source)
XLA Modules:
  0.0 303.1 jit_solution(9531522630871206582)
XLA Ops:
  9.0 7.0 %fusion.9 = bf16[256,4096]{1,0:T(8,128)(2,1)} fusion(bf16[256,1024]{1,0:T(8,128)(2,1)S(1)} %copy-done, bf16[2,1024,4096]{2,1,0:T(8,128)(2,1)} %param.12), kind=kOutput, calls=%fused_computation.7 | convolution fusion | flops 2148532224 | bytes 11010048 | tf_op jit(solution)/shard_map/dot_general | solution.py:22
  17.7 2.0 reshape.39
  19.8 3.4 %fusion.23 = f32[16,12,4,4]{0,3,2,1:T(4,128)S(1)} fusion(bf16[16,12,4,1024]{3,2,1,0:T(4,128)(2,1)} %reshape.39, bf16[2,12,4,1024]{3,2,1,0:T(4,128)(2,1)S(1)} %copy-done.8), kind=kOutput, calls=%fused_computation.32 | convolution fusion | flops 6291456 | bytes 1683456 | tf_op jit(solution)/shard_map/tmsd,mrd->tmsr/dot_general | solution.py:30
  23.1 14.2 %psum.35 = f32[16,12,4,4]{0,3,2,1:T(4,128)S(1)} all-reduce(f32[16,12,4,4]{0,3,2,1:T(4,128)S(1)} %fusion.23), channel_id=1, replica_groups=mesh['pop'=8,'mp'=4] {'mp'}, use_global_device_ids=true, to_apply=%region_1.0 | all-reduce | flops 3072 | bytes 24576 | tf_op jit(solution)/shard_map/psum | solution.py:74
  37.4 3.1 %convolution_multiply_fusion.1 = f32[12,1024,16,4]{1,2,3,0:T(8,128)} fusion(f32[16,12,4,4]{0,3,2,1:T(4,128)S(1)} %psum.35, bf16[2,12,4,4096]{3,2,1,0:T(4,128)(2,1)S(1)} %copy-done.7, s32[]{:T(128)S(6)} %select_n.3), kind=kOutput, calls=%fused_computation.21 | convolution fusion | flops 38535168 | bytes 3342340 | tf_op jit(solution)/shard_map/tmsr,mrd->tmsd/dot_general | solution.py:75
  40.5 9.7 %reduce-scatter.3.cloned.1.call-done = bf16[256,1024]{1,0:T(8,128)(2,1)} async-done(((bf16[256,4096]{1,0:T(8,128)(2,1)}), bf16[256,1024]{1,0:T(8,128)(2,1)}) %reduce-scatter.3.cloned.1.call-update) | async-done | bytes 524304 | tf_op jit(solution)/shard_map/reduce_scatter | solution.py:23
  51.9 2.3 convolution_add_fusion
  54.2 4.8 %reshape.40 = f32[16,12,4,1024]{3,2,1,0:T(4,128)} reshape(f32[768,1024]{1,0:T(8,128)} %convolution_add_fusion) | data formatting | bytes 6291456 | tf_op jit(solution)/shard_map/reshape | solution.py:73
  59.0 5.3 %fusion.13 = f32[16,12,4,1024]{3,2,1,0:T(4,128)S(1)} fusion(f32[16,12,4,1024]{3,2,1,0:T(4,128)} %reshape.40, f32[12,1024,16,4]{1,2,3,0:T(8,128)} %convolution_multiply_fusion.1), kind=kLoop, calls=%fused_computation.12 | loop fusion | flops 786432 | bytes 9437184 | tf_op jit(solution)/shard_map/add | solution.py:78
  78.2 1.8 constant_dynamic-update-slice_fusion.5
  90.4 4.9 %stack.7 = f32[768,1024]{1,0:T(8,128)} reshape(f32[16,12,4,1024]{3,2,1,0:T(4,128)} %fusion.52) | data formatting | bytes 6291456 | tf_op jit(solution)/shard_map/stack | solution.py:17
  95.3 2.6 multiply_reduce_fusion.1
  98.1 10.7 %psum.36 = f32[16,12,4]{0,2,1:T(4,128)S(1)} all-reduce(f32[16,12,4]{0,2,1:T(4,128)S(1)} %copy.84), channel_id=1, replica_groups=mesh['pop'=8,'mp'=4] {'mp'}, use_global_device_ids=true, to_apply=%region_3.0 | all-reduce | flops 768 | bytes 6144 | tf_op jit(solution)/shard_map/psum | solution.py:79
  109.0 12.7 %fusion.6 = bf16[768,4096]{1,0:T(8,128)(2,1)} fusion(bf16[2,1024,4096]{2,1,0:T(8,128)(2,1)} %param.12, f32[768,1024]{1,0:T(8,128)} %stack.7, bf16[768,1024]{1,0:T(8,128)(2,1)S(1)} %convolution_convert_fusion, f32[1024]{0:T(1024)S(1)} %bitcast.112, f32[768]{0:T(1024)S(1)} %mul.1061), kind=kOutput, calls=%fused_computation.6 | convolution fusion | flops 6449528832 | bytes 19405824 | tf_op jit(solution)/shard_map/dot_general | solution.py:22
  121.8 9.1 %copy.71 = bf16[2,12,4,4096]{1,2,0,3:T(4,128)(2,1)} copy(bf16[2,12,4,4096]{3,2,1,0:T(4,128)(2,1)S(1)} %copy-done.7) | data formatting | bytes 1572864 | tf_op args[5]
  130.9 17.7 %reshape.57 = bf16[8,2,24576]{2,1,0:T(2,128)(2,1)} reshape(bf16[4096,2,4,12]{3,2,1,0:T(4,128)(2,1)} %bitcast.75) | data formatting | bytes 1572864
  148.6 5.7 %all-to-all-start = ((bf16[8,2,24576]{2,1,0:T(2,128)(2,1)}), bf16[8,2,24576]{2,1,0:T(2,128)(2,1)S(1)}, u32[]{:S(2)}, u32[]{:S(2)}) async-start(bf16[8,2,24576]{2,1,0:T(2,128)(2,1)} %reshape.57), calls=%async_computation.2 | async-start | bytes 1572864 | tf_op jit(solution)/shard_map/all_to_all | solution.py:95
  155.9 19.1 %all-reduce = s32[96]{0:T(128)S(1)} all-reduce(s32[96]{0:T(128)S(1)} %dynamic-update-slice), channel_id=1, replica_groups=mesh['pop'=8,'mp'=4] {'pop'}, use_global_device_ids=true, to_apply=%add | all-reduce | flops 96 | bytes 768
  177.5 20.4 %reshape.58 = bf16[4096,2,4,12]{3,2,1,0:T(4,128)(2,1)} reshape(bf16[8,2,24576]{2,1,0:T(2,128)(2,1)S(1)} %all-to-all-done) | data formatting | bytes 1572864
  197.9 12.0 %copy.72 = bf16[2,12,4,8,512]{4,2,1,3,0:T(4,128)(2,1)S(1)} copy(bf16[2,12,4,8,512]{1,2,0,4,3:T(4,128)(2,1)} %bitcast.74) | data formatting | bytes 1572864 | tf_op jit(solution)/shard_map/all_to_all | solution.py:95
  210.0 2.1 multiply_convert_fusion
  212.1 3.4 %bitcast_multiply_fusion = f32[2,1024,512]{2,1,0:T(8,128)} fusion(bf16[2,96,4,1024]{3,2,1,0:T(4,128)(2,1)S(1)} %multiply_convert_fusion, bf16[2,96,4,512]{3,2,1,0:T(4,128)(2,1)S(1)} %bitcast.76), kind=kOutput, calls=%fused_computation.8 | convolution fusion | flops 806354944 | bytes 6553600 | tf_op jit(solution)/shard_map/lmri,lmro->lio/dot_general | solution.py:100
  215.5 3.0 %add_convert_fusion.2 = bf16[16,12,4,1024]{3,2,1,0:T(4,128)(2,1)S(1)} fusion(f32[16,12,4,1024]{3,2,1,0:T(4,128)} %fusion.52, bf16[16,12,4,1024]{3,2,1,0:T(4,128)(2,1)S(1)} %copy-done.5, f32[1024]{0:T(1024)S(1)} %bitcast.113, f32[16,12,4]{2,1,0:T(8,128)S(1)} %copy.65), kind=kLoop, calls=%fused_computation.17 | loop fusion | flops 3932160 | bytes 6298624 | tf_op jit(solution)/shard_map/convert_element_type | solution.py:83
  218.6 1.9 fusion.26
  220.5 11.7 %psum.37 = f32[16,12,4,4]{0,3,2,1:T(4,128)S(1)} all-reduce(f32[16,12,4,4]{0,3,2,1:T(4,128)S(1)} %fusion.26), channel_id=1, replica_groups=mesh['pop'=8,'mp'=4] {'mp'}, use_global_device_ids=true, to_apply=%region_5.0 | all-reduce | flops 3072 | bytes 24576 | tf_op jit(solution)/shard_map/psum | solution.py:74
  232.2 3.1 %convolution_multiply_fusion = f32[12,1024,16,4]{1,2,3,0:T(8,128)} fusion(f32[16,12,4,4]{0,3,2,1:T(4,128)S(1)} %psum.37, bf16[2,12,4,4096]{3,2,1,0:T(4,128)(2,1)S(1)} %copy-done.7, s32[]{:T(128)S(6)} %add.456, s32[]{:T(128)S(6)} %select_n.3), kind=kOutput, calls=%fused_computation.20 | convolution fusion | flops 38535168 | bytes 3342344 | tf_op jit(solution)/shard_map/tmsr,mrd->tmsd/dot_general | solution.py:75
  235.3 4.1 %reshape.44 = f32[16,12,4,1024]{3,2,1,0:T(4,128)} reshape(bf16[768,1024]{1,0:T(8,128)(2,1)} %reduce-scatter.5.cloned.1.call-done) | data formatting | bytes 4718592 | tf_op jit(solution)/shard_map/reshape | solution.py:73
  239.4 5.3 %fusion.12 = f32[16,12,4,1024]{3,2,1,0:T(4,128)S(1)} fusion(f32[16,12,4,1024]{3,2,1,0:T(4,128)} %reshape.44, f32[12,1024,16,4]{1,2,3,0:T(8,128)} %convolution_multiply_fusion), kind=kLoop, calls=%fused_computation.10 | loop fusion | flops 786432 | bytes 9437184 | tf_op jit(solution)/shard_map/add | solution.py:78
  264.0 10.5 %psum.38 = f32[16,12,4]{0,2,1:T(4,128)S(1)} all-reduce(f32[16,12,4]{0,2,1:T(4,128)S(1)} %copy.85), channel_id=1, replica_groups=mesh['pop'=8,'mp'=4] {'mp'}, use_global_device_ids=true, to_apply=%region_7.0 | all-reduce | flops 768 | bytes 6144 | tf_op jit(solution)/shard_map/psum | solution.py:79
  274.8 3.1 %add_convert_fusion = bf16[16,12,4,1024]{3,2,1,0:T(4,128)(2,1)S(1)} fusion(f32[16,12,4,1024]{3,2,1,0:T(4,128)} %copy-done.4, bf16[16,12,4,1024]{3,2,1,0:T(4,128)(2,1)S(1)} %add_convert_fusion.2, f32[1024]{0:T(1024)S(1)} %bitcast.111, f32[16,12,4]{2,1,0:T(8,128)S(1)} %copy.70), kind=kLoop, calls=%fused_computation.14 | loop fusion | flops 3932160 | bytes 6298624 | tf_op jit(solution)/shard_map/convert_element_type | solution.py:83
  278.5 5.6 %fusion.14 = f32[1,16,12,4]{1,0,3,2:T(1,128)S(1)} fusion(f32[1024,1,1,1]{0,1,3,2:T(1,128)S(1)} %bitcast.114, bf16[16,12,4,1024]{3,2,1,0:T(4,128)(2,1)S(1)} %add_convert_fusion), kind=kOutput, calls=%fused_computation.23 | convolution fusion | flops 9437184 | bytes 1580032 | tf_op jit(solution)/shard_map/tmsd,d->tms/dot_general | solution.py:84
  284.1 10.6 %psum.39 = f32[16,12,4]{0,2,1:T(4,128)S(1)} all-reduce(f32[16,12,4]{0,2,1:T(4,128)S(1)} %bitcast.110), channel_id=1, replica_groups=mesh['pop'=8,'mp'=4] {'mp'}, use_global_device_ids=true, to_apply=%region_8.0 | all-reduce | flops 768 | bytes 6144 | tf_op jit(solution)/shard_map/psum | solution.py:87
  (96 shorter events, 51.9 us)
Async XLA Ops:
  8.0 1.1 copy-start
  8.0 8.7 %copy-start.10 = (f32[2,1024]{1,0:T(2,128)S(1)}, f32[2,1024]{1,0:T(2,128)}, u32[]{:S(2)}) copy-start(f32[2,1024]{1,0:T(2,128)} %param.15) | copy-start | bytes 24580
  8.0 8.8 %copy-start.11 = (f32[2,1024]{1,0:T(2,128)S(1)}, f32[2,1024]{1,0:T(2,128)}, u32[]{:S(2)}) copy-start(f32[2,1024]{1,0:T(2,128)} %param.16) | copy-start | bytes 24580
  8.0 8.8 %copy-start.9 = (s32[12,4,16]{2,1,0:T(4,128)S(1)}, s32[12,4,16]{2,1,0:T(4,128)}, u32[]{:S(2)}) copy-start(s32[12,4,16]{2,1,0:T(4,128)} %param.9) | copy-start | bytes 9220
  8.0 42.1 %reduce-scatter.3.cloned.1.call-start = ((), (), s32[]{:S(2)}) async-start(), calls=%async_computation.3 | async-start | bytes 2621440 | tf_op jit(solution)/shard_map/reduce_scatter | solution.py:23
  16.1 3.6 %copy-start.8 = (bf16[2,12,4,1024]{3,2,1,0:T(4,128)(2,1)S(1)}, bf16[2,12,4,1024]{3,2,1,0:T(4,128)(2,1)}, u32[]{:S(2)}) copy-start(bf16[2,12,4,1024]{3,2,1,0:T(4,128)(2,1)} %param.13) | copy-start | bytes 589828
  16.1 193.8 %all-gather.2.cloned.1.call-start = ((), (), s32[]{:S(2)}) async-start(), calls=%async_computation.5 | async-start | bytes 1769472 | tf_op jit(solution)/shard_map/all_gather | solution.py:97
  16.7 218.6 %reduce-scatter.5.cloned.1.call-start = ((), (), s32[]{:S(2)}) async-start(), calls=%async_computation.4 | async-start | bytes 7864320 | tf_op jit(solution)/shard_map/reduce_scatter | solution.py:23
  17.7 19.6 %copy-start.7 = (bf16[2,12,4,4096]{3,2,1,0:T(4,128)(2,1)S(1)}, bf16[2,12,4,4096]{3,2,1,0:T(4,128)(2,1)}, u32[]{:S(2)}) copy-start(bf16[2,12,4,4096]{3,2,1,0:T(4,128)(2,1)} %param.14) | copy-start | bytes 2359300
  50.2 1.7 copy-start.6
  64.3 1.8 copy-start.2
  130.9 23.5 %copy-start.14 = (u32[32]{0:T(128)S(1)}, u32[32]{0:T(128)}, u32[]{:S(2)}) copy-start(u32[32]{0:T(128)} %constant.44) | copy-start | bytes 388
  130.9 24.7 %copy-start.13 = (s32[12]{0:T(128)S(1)}, s32[12]{0:T(128)}, u32[]{:S(2)}) copy-start(s32[12]{0:T(128)} %param.10) | copy-start | bytes 148
  148.6 28.9 %all-to-all-start = ((bf16[8,2,24576]{2,1,0:T(2,128)(2,1)}), bf16[8,2,24576]{2,1,0:T(2,128)(2,1)S(1)}, u32[]{:S(2)}, u32[]{:S(2)}) async-start(bf16[8,2,24576]{2,1,0:T(2,128)(2,1)} %reshape.57), calls=%async_computation.2 | async-start | bytes 1572864 | tf_op jit(solution)/shard_map/all_to_all | solution.py:95
  212.1 3.5 %copy-start.5 = (bf16[16,12,4,1024]{3,2,1,0:T(4,128)(2,1)S(1)}, bf16[16,12,4,1024]{3,2,1,0:T(4,128)(2,1)}, u32[]{:S(2)}) copy-start(bf16[16,12,4,1024]{3,2,1,0:T(4,128)(2,1)} %reshape.39) | copy-start | bytes 4718596
  244.7 1.7 copy-start.3
  261.5 1.7 copy-start.4
  274.7 20.7 %copy-start.1 = (bf16[256,1024]{1,0:T(8,128)(2,1)S(1)}, bf16[256,1024]{1,0:T(8,128)(2,1)}, u32[]{:S(2)}) copy-start(bf16[256,1024]{1,0:T(8,128)(2,1)} %param.11) | copy-start | bytes 1572868
  274.7 3.7 %copy-start.12 = (f32[1024]{0:T(1024)S(1)}, f32[1024]{0:T(1024)}, u32[]{:S(2)}) copy-start(f32[1024]{0:T(1024)} %param.17) | copy-start | bytes 12292
Sparse Core Ops, SparseCore 0:
  16.2 33.8 reduce-scatter.2
  121.9 58.4 reduce-scatter.4
Sparse Core Ops, SparseCore 1:
  18.8 46.8 all-gather.1
where the time goes:
time: 308 us; the launch traced here: 303 us
  local copies, waits for them, and re-layouts  82.4 us (27%)
  blocking collectives  76.8 us (25%)
  other arithmetic  64.7 us (21%)
  matrix products  45 us (15%)
  between operations  18.1 us (6%)
  waiting for transfers between devices  10.3 us (3%)
  starting transfers between devices  5.86 us (2%)
    unnamed x39, local copies, waits for them, and re-layouts  53.2 us
    unnamed x30, other arithmetic  38.4 us
    psum x2, blocking collectives, shards(): low_rank = lax.psum(project_rank(hidden, factors_in[layer_idx]), 'mp')  25.9 us
    psum x2, blocking collectives, shards(): squares = lax.psum(jnp.sum(states * states, axis=3), 'mp')  21.2 us
    dot_general x2, matrix products, mixed_inputs(): jnp.dot(flat, weight_rows, preferred_element_type=jnp.float32)  19.8 us
    unnamed x1, blocking collectives  19.1 us
    all_to_all x1, local copies, waits for them, and re-layouts, shards(): lax.all_to_all(factors_out, 'pop', split_axis=3, concat_axis=1, tiled=True)  12 us
    psum x1, blocking collectives, shards(): reward_terms = lax.psum(dots_local, 'mp')  10.6 us
  transfers between devices with their start and end apart: 4, of which 1 were waited for; matrix products, arithmetic and copies ran while one was open for 48% of the time, Pallas kernels for 0%

commit v1 on v0

--- a/solution.py
+++ b/solution.py
@@ -92,7 +92,12 @@
     rank_mean = jnp.mean(shares_all)
     rank_spread = jnp.mean((shares_all - rank_mean) * (shares_all - rank_mean)) + spread_eps
     shaped_all = (shares_all - rank_mean) * lax.rsqrt(rank_spread)
-    columns = lax.all_to_all(factors_out, "pop", split_axis=3, concat_axis=1, tiled=True)
+    columns = jnp.concatenate(
+        lax.all_to_all(
+            jnp.stack(jnp.split(factors_out, lax.axis_size("pop"), axis=3)), "pop", 0, 0
+        ),
+        axis=1,
+    )
     weighted = (
         lax.all_gather(factors_in, "pop", axis=1, tiled=True).astype(jnp.float32)
         * shaped_all[None, :, None, None]

time: 308 us -> 235 us (0.76); the launches traced: 303 us -> 234 us
  local copies, waits for them, and re-layouts: 82.4 us -> 33.5 us
  other arithmetic: 64.7 us -> 48.1 us
    unnamed x39 -> x45, local copies, waits for them, and re-layouts: 53.2 us -> 16.5 us
    unnamed x30, other arithmetic: 38.4 us -> 25.6 us
    all_to_all x1 -> x0, local copies, waits for them, and re-layouts: 12 us -> none  [shards(): lax.all_to_all(factors_out, 'pop', split_axis=3, concat_axis=1, tiled=True)]
  transfers between devices with their start and end apart: 4 -> 4, of which waited for: 1 -> 1; matrix products, arithmetic and copies ran while one was open for 48% -> 35% of each run, Pallas kernels for 0% -> 0%
where the time goes in v1:
time: 235 us; the launch traced here: 234 us
  blocking collectives  75.4 us (32%)
  other arithmetic  48.1 us (20%)
  matrix products  43.6 us (19%)
  local copies, waits for them, and re-layouts  33.5 us (14%)
  between operations  17.9 us (8%)
  waiting for transfers between devices  9.34 us (4%)
  starting transfers between devices  5.68 us (2%)
    psum x2, blocking collectives, shards(): low_rank = lax.psum(project_rank(hidden, factors_in[layer_idx]), 'mp')  25.8 us
    unnamed x30, other arithmetic  25.6 us
    psum x2, blocking collectives, shards(): squares = lax.psum(jnp.sum(states * states, axis=3), 'mp')  20.7 us
    dot_general x2, matrix products, mixed_inputs(): jnp.dot(flat, weight_rows, preferred_element_type=jnp.float32)  20 us
    unnamed x1, blocking collectives  18.7 us
    unnamed x45, local copies, waits for them, and re-layouts  16.5 us
    psum x1, blocking collectives, shards(): reward_terms = lax.psum(dots_local, 'mp')  10.3 us
    add x2, other arithmetic, shards(): states = recurrence(base_mix + coef * correction, decay_rates[layer_idx])  9.61 us
  transfers between devices with their start and end apart: 4, of which 1 were waited for; matrix products, arithmetic and copies ran while one was open for 35% of the time, Pallas kernels for 0%

profile of v1, /device:TPU:0, one launch (start us, length us, event | category | flops | bytes accessed | tf_op | source)
XLA Modules:
  0.0 233.5 jit_solution(15376411211532444951)
XLA Ops:
  9.0 7.0 %fusion.9 = bf16[256,4096]{1,0:T(8,128)(2,1)} fusion(bf16[256,1024]{1,0:T(8,128)(2,1)S(1)} %copy-done, bf16[2,1024,4096]{2,1,0:T(8,128)(2,1)} %param.12), kind=kOutput, calls=%fused_computation.7 | convolution fusion | flops 2148532224 | bytes 11010048 | tf_op jit(solution)/shard_map/dot_general | solution.py:22
  17.7 2.3 reshape.45
  20.0 3.4 %fusion.23 = f32[16,12,4,4]{0,3,2,1:T(4,128)S(1)} fusion(bf16[16,12,4,1024]{3,2,1,0:T(4,128)(2,1)} %reshape.45, bf16[2,12,4,1024]{3,2,1,0:T(4,128)(2,1)S(1)} %copy-done.9), kind=kOutput, calls=%fused_computation.32 | convolution fusion | flops 6291456 | bytes 1683456 | tf_op jit(solution)/shard_map/tmsd,mrd->tmsr/dot_general | solution.py:30
  23.3 14.0 %psum.35 = f32[16,12,4,4]{0,3,2,1:T(4,128)S(1)} all-reduce(f32[16,12,4,4]{0,3,2,1:T(4,128)S(1)} %fusion.23), channel_id=1, replica_groups=mesh['pop'=8,'mp'=4] {'mp'}, use_global_device_ids=true, to_apply=%region_1.0 | all-reduce | flops 3072 | bytes 24576 | tf_op jit(solution)/shard_map/psum | solution.py:74
  37.4 4.0 %convolution_multiply_fusion.1 = f32[12,1024,16,4]{1,2,3,0:T(8,128)} fusion(f32[16,12,4,4]{0,3,2,1:T(4,128)S(1)} %psum.35, bf16[2,12,4,4096]{3,2,1,0:T(4,128)(2,1)} %param.14, s32[]{:T(128)S(6)} %select_n.3), kind=kOutput, calls=%fused_computation.21 | convolution fusion | flops 38535168 | bytes 3256324 | tf_op jit(solution)/shard_map/tmsr,mrd->tmsd/dot_general | solution.py:75
  41.4 8.8 %reduce-scatter.3.cloned.1.call-done = bf16[256,1024]{1,0:T(8,128)(2,1)} async-done(((bf16[256,4096]{1,0:T(8,128)(2,1)}), bf16[256,1024]{1,0:T(8,128)(2,1)}) %reduce-scatter.3.cloned.1.call-update) | async-done | bytes 524304 | tf_op jit(solution)/shard_map/reduce_scatter | solution.py:23
  50.2 1.7 fusion.30
  52.6 2.6 %reshape.46 = f32[16,12,4,1024]{3,2,1,0:T(4,128)} reshape(f32[768,1024]{1,0:T(8,128)S(1)} %convolution_add_fusion) | data formatting | bytes 6291456 | tf_op jit(solution)/shard_map/reshape | solution.py:73
  55.1 5.3 %fusion.13 = f32[16,12,4,1024]{3,2,1,0:T(4,128)S(1)} fusion(f32[16,12,4,1024]{3,2,1,0:T(4,128)} %reshape.46, f32[12,1024,16,4]{1,2,3,0:T(8,128)} %convolution_multiply_fusion.1), kind=kLoop, calls=%fused_computation.12 | loop fusion | flops 786432 | bytes 9437184 | tf_op jit(solution)/shard_map/add | solution.py:78
  77.2 2.7 %stack.25 = f32[768,1024]{1,0:T(8,128)} reshape(f32[16,12,4,1024]{3,2,1,0:T(4,128)S(1)} %fusion.52) | data formatting | bytes 6291456 | tf_op jit(solution)/shard_map/stack | solution.py:17
  80.7 10.5 %psum.36 = f32[16,12,4]{0,2,1:T(4,128)S(1)} all-reduce(f32[16,12,4]{0,2,1:T(4,128)S(1)} %copy.70), channel_id=1, replica_groups=mesh['pop'=8,'mp'=4] {'mp'}, use_global_device_ids=true, to_apply=%region_3.0 | all-reduce | flops 768 | bytes 6144 | tf_op jit(solution)/shard_map/psum | solution.py:79
  91.5 12.9 %fusion.6 = bf16[768,4096]{1,0:T(8,128)(2,1)} fusion(bf16[2,1024,4096]{2,1,0:T(8,128)(2,1)} %param.12, f32[768,1024]{1,0:T(8,128)} %stack.25, bf16[768,1024]{1,0:T(8,128)(2,1)} %copy-done.3, f32[1024]{0:T(1024)S(1)} %bitcast.122, f32[768]{0:T(1024)S(1)} %mul.1061), kind=kOutput, calls=%fused_computation.6 | convolution fusion | flops 6449528832 | bytes 19405824 | tf_op jit(solution)/shard_map/dot_general | solution.py:22
  104.5 1.6 bitcast_dynamic-update-slice_fusion.7
  110.8 1.6 bitcast_dynamic-update-slice_fusion.3
  112.3 1.6 bitcast_dynamic-update-slice_fusion.2
  113.9 1.6 bitcast_dynamic-update-slice_fusion.1
  115.5 1.6 bitcast_dynamic-update-slice_fusion
  117.1 5.6 %all-to-all-start = ((bf16[8,2,12,4,512]{4,3,2,1,0:T(4,128)(2,1)}), bf16[8,2,12,4,512]{4,3,2,1,0:T(4,128)(2,1)}, u32[]{:S(2)}, u32[]{:S(2)}) async-start(bf16[8,2,12,4,512]{4,3,2,1,0:T(4,128)(2,1)} %bitcast_dynamic-update-slice_fusion), calls=%async_computation.2 | async-start | bytes 1572864 | tf_op jit(solution)/shard_map/all_to_all | solution.py:96
  124.2 18.7 %all-reduce = s32[96]{0:T(128)S(1)} all-reduce(s32[96]{0:T(128)S(1)} %dynamic-update-slice), channel_id=1, replica_groups=mesh['pop'=8,'mp'=4] {'pop'}, use_global_device_ids=true, to_apply=%add | all-reduce | flops 96 | bytes 768
  145.4 2.3 %copy.58 = bf16[2,8,12,4,512]{4,3,2,1,0:T(4,128)(2,1)} copy(bf16[2,8,12,4,512]{4,3,2,0,1:T(4,128)(2,1)} %bitcast.37) | data formatting | bytes 1572864 | tf_op jit(solution)/shard_map/reshape | solution.py:95
  147.8 2.2 multiply_convert_fusion
  149.9 3.4 %bitcast_multiply_fusion = f32[2,1024,512]{2,1,0:T(8,128)} fusion(bf16[2,96,4,1024]{3,2,1,0:T(4,128)(2,1)S(1)} %multiply_convert_fusion, bf16[2,96,4,512]{3,2,1,0:T(4,128)(2,1)S(1)} %bitcast.86), kind=kOutput, calls=%fused_computation.8 | convolution fusion | flops 806354944 | bytes 6553600 | tf_op jit(solution)/shard_map/lmri,lmro->lio/dot_general | solution.py:105
  155.7 1.9 fusion.26
  157.6 11.8 %psum.37 = f32[16,12,4,4]{0,3,2,1:T(4,128)S(1)} all-reduce(f32[16,12,4,4]{0,3,2,1:T(4,128)S(1)} %fusion.26), channel_id=1, replica_groups=mesh['pop'=8,'mp'=4] {'mp'}, use_global_device_ids=true, to_apply=%region_5.0 | all-reduce | flops 3072 | bytes 24576 | tf_op jit(solution)/shard_map/psum | solution.py:74
  169.4 2.3 %convolution_multiply_fusion = f32[12,1024,16,4]{1,2,3,0:T(8,128)S(1)} fusion(f32[16,12,4,4]{0,3,2,1:T(4,128)S(1)} %psum.37, bf16[2,12,4,4096]{3,2,1,0:T(4,128)(2,1)} %param.14, s32[]{:T(128)S(6)} %add.456, s32[]{:T(128)S(6)} %select_n.3), kind=kOutput, calls=%fused_computation.20 | convolution fusion | flops 38535168 | bytes 3256328 | tf_op jit(solution)/shard_map/tmsr,mrd->tmsd/dot_general | solution.py:75
  171.8 4.1 %reshape.52 = f32[16,12,4,1024]{3,2,1,0:T(4,128)} reshape(bf16[768,1024]{1,0:T(8,128)(2,1)} %reduce-scatter.5.cloned.1.call-done) | data formatting | bytes 4718592 | tf_op jit(solution)/shard_map/reshape | solution.py:73
  175.9 4.3 %fusion.12 = f32[16,12,4,1024]{3,2,1,0:T(4,128)S(1)} fusion(f32[16,12,4,1024]{3,2,1,0:T(4,128)} %reshape.52, f32[12,1024,16,4]{1,2,3,0:T(8,128)S(1)} %convolution_multiply_fusion), kind=kLoop, calls=%fused_computation.10 | loop fusion | flops 786432 | bytes 9437184 | tf_op jit(solution)/shard_map/add | solution.py:78
  192.5 2.6 %multiply_reduce_fusion = f32[16,12,4]{2,1,0:T(8,128)S(1)} fusion(f32[16,12,4,1024]{3,2,1,0:T(4,128)} %fusion.35), kind=kLoop, calls=%fused_computation.15 | loop fusion | flops 1572096 | bytes 3148800 | tf_op jit(solution)/shard_map/reduce_sum | solution.py:79
  195.2 10.3 %psum.38 = f32[16,12,4]{0,2,1:T(4,128)S(1)} all-reduce(f32[16,12,4]{0,2,1:T(4,128)S(1)} %copy.71), channel_id=1, replica_groups=mesh['pop'=8,'mp'=4] {'mp'}, use_global_device_ids=true, to_apply=%region_7.0 | all-reduce | flops 768 | bytes 6144 | tf_op jit(solution)/shard_map/psum | solution.py:79
  205.7 3.0 %add_convert_fusion = bf16[16,12,4,1024]{3,2,1,0:T(4,128)(2,1)S(1)} fusion(f32[16,12,4,1024]{3,2,1,0:T(4,128)} %fusion.35, bf16[16,12,4,1024]{3,2,1,0:T(4,128)(2,1)S(1)} %copy-done.6, f32[1024]{0:T(1024)S(1)} %bitcast.121, f32[16,12,4]{2,1,0:T(8,128)S(1)} %copy.57), kind=kLoop, calls=%fused_computation.14 | loop fusion | flops 3932160 | bytes 6298624 | tf_op jit(solution)/shard_map/convert_element_type | solution.py:83
  209.5 5.6 %fusion.14 = f32[1,16,12,4]{1,0,3,2:T(1,128)S(1)} fusion(f32[1024,1,1,1]{0,1,3,2:T(1,128)S(1)} %bitcast.124, bf16[16,12,4,1024]{3,2,1,0:T(4,128)(2,1)S(1)} %add_convert_fusion), kind=kOutput, calls=%fused_computation.23 | convolution fusion | flops 9437184 | bytes 1580032 | tf_op jit(solution)/shard_map/tmsd,d->tms/dot_general | solution.py:84
  215.0 10.3 %psum.39 = f32[16,12,4]{0,2,1:T(4,128)S(1)} all-reduce(f32[16,12,4]{0,2,1:T(4,128)S(1)} %bitcast.120), channel_id=1, replica_groups=mesh['pop'=8,'mp'=4] {'mp'}, use_global_device_ids=true, to_apply=%region_8.0 | all-reduce | flops 768 | bytes 6144 | tf_op jit(solution)/shard_map/psum | solution.py:87
  (103 shorter events, 44.2 us)
Async XLA Ops:
  8.0 1.1 copy-start
  8.0 8.7 %copy-start.10 = (s32[12,4,16]{2,1,0:T(4,128)S(1)}, s32[12,4,16]{2,1,0:T(4,128)}, u32[]{:S(2)}) copy-start(s32[12,4,16]{2,1,0:T(4,128)} %param.9) | copy-start | bytes 9220
  8.0 42.1 %reduce-scatter.3.cloned.1.call-start = ((), (), s32[]{:S(2)}) async-start(), calls=%async_computation.3 | async-start | bytes 2621440 | tf_op jit(solution)/shard_map/reduce_scatter | solution.py:23
  16.1 3.9 %copy-start.9 = (bf16[2,12,4,1024]{3,2,1,0:T(4,128)(2,1)S(1)}, bf16[2,12,4,1024]{3,2,1,0:T(4,128)(2,1)}, u32[]{:S(2)}) copy-start(bf16[2,12,4,1024]{3,2,1,0:T(4,128)(2,1)} %param.13) | copy-start | bytes 589828
  16.1 131.6 %all-gather.2.cloned.1.call-start = ((), (), s32[]{:S(2)}) async-start(), calls=%async_computation.5 | async-start | bytes 1769472 | tf_op jit(solution)/shard_map/all_gather | solution.py:102
  16.7 155.1 %reduce-scatter.5.cloned.1.call-start = ((), (), s32[]{:S(2)}) async-start(), calls=%async_computation.4 | async-start | bytes 7864320 | tf_op jit(solution)/shard_map/reduce_scatter | solution.py:23
  17.7 23.7 %copy-start.3 = (bf16[768,1024]{1,0:T(8,128)(2,1)}, bf16[768,1024]{1,0:T(8,128)(2,1)S(1)}, u32[]{:S(2)}) copy-start(bf16[768,1024]{1,0:T(8,128)(2,1)S(1)} %convolution_convert_fusion) | copy-start | bytes 4718596
  17.7 19.7 %copy-start.11 = (f32[2,1024]{1,0:T(2,128)S(1)}, f32[2,1024]{1,0:T(2,128)}, u32[]{:S(2)}) copy-start(f32[2,1024]{1,0:T(2,128)} %param.15) | copy-start | bytes 24580
  17.7 19.7 %copy-start.12 = (f32[2,1024]{1,0:T(2,128)S(1)}, f32[2,1024]{1,0:T(2,128)}, u32[]{:S(2)}) copy-start(f32[2,1024]{1,0:T(2,128)} %param.16) | copy-start | bytes 24580
  50.2 1.7 copy-start.8
  60.4 1.7 copy-start.2
  104.4 18.2 %copy-start.15 = (u32[32]{0:T(128)S(1)}, u32[32]{0:T(128)}, u32[]{:S(2)}) copy-start(u32[32]{0:T(128)} %constant.44) | copy-start | bytes 388
  104.5 19.4 %copy-start.14 = (s32[12]{0:T(128)S(1)}, s32[12]{0:T(128)}, u32[]{:S(2)}) copy-start(s32[12]{0:T(128)} %param.10) | copy-start | bytes 148
  117.1 28.3 %all-to-all-start = ((bf16[8,2,12,4,512]{4,3,2,1,0:T(4,128)(2,1)}), bf16[8,2,12,4,512]{4,3,2,1,0:T(4,128)(2,1)}, u32[]{:S(2)}, u32[]{:S(2)}) async-start(bf16[8,2,12,4,512]{4,3,2,1,0:T(4,128)(2,1)} %bitcast_dynamic-update-slice_fusion), calls=%async_computation.2 | async-start | bytes 1572864 | tf_op jit(solution)/shard_map/all_to_all | solution.py:96
  147.8 2.2 copy-start.7
  149.9 3.5 %copy-start.4 = (bf16[16,12,4,1024]{3,2,1,0:T(4,128)(2,1)S(1)}, bf16[16,12,4,1024]{3,2,1,0:T(4,128)(2,1)}, u32[]{:S(2)}) copy-start(bf16[16,12,4,1024]{3,2,1,0:T(4,128)(2,1)} %reshape.45) | copy-start | bytes 4718596
  154.6 1.1 copy-start.5
  190.2 15.5 %copy-start.6 = (bf16[16,12,4,1024]{3,2,1,0:T(4,128)(2,1)S(1)}, bf16[16,12,4,1024]{3,2,1,0:T(4,128)(2,1)}, u32[]{:S(2)}) copy-start(bf16[16,12,4,1024]{3,2,1,0:T(4,128)(2,1)} %copy-done.5) | copy-start | bytes 4718596
  205.7 20.4 %copy-start.1 = (bf16[256,1024]{1,0:T(8,128)(2,1)S(1)}, bf16[256,1024]{1,0:T(8,128)(2,1)}, u32[]{:S(2)}) copy-start(bf16[256,1024]{1,0:T(8,128)(2,1)} %param.11) | copy-start | bytes 1572868
  205.7 3.7 %copy-start.13 = (f32[1024]{0:T(1024)S(1)}, f32[1024]{0:T(1024)}, u32[]{:S(2)}) copy-start(f32[1024]{0:T(1024)} %param.17) | copy-start | bytes 12292
Sparse Core Ops, SparseCore 0:
  16.2 33.8 reduce-scatter.2
  104.6 58.2 reduce-scatter.4
Sparse Core Ops, SparseCore 1:
  18.8 46.8 all-gather.1
